TPU v7x, 1024 devices: a whole 4x8x16 slice. The times are simulated.
1024 devices in a mesh: edp: 16 (over z), ep: 64 (over y, x, core).
Axes of the slice: x: 4, y: 8, z: 16, core: 2. Of those that a mesh axis runs over, the one named last changes fastest.
Arguments:
- out_grad: bfloat16 [131072, 3584], P(('edp', 'ep')), may hold values from -0.59765625 to 0.59765625
- routes: int32 [131072, 8], P(('edp', 'ep')), may hold values from 0 to 383, as said below
- gate_weights: float32 [131072, 8], P(('edp', 'ep')), may hold values from 0.02 to 0.5
- hidden: bfloat16 [8192, 16384], P('edp', 'ep'), may hold values from -6 to 6
Outputs:
- weight_grad: float32 [3584, 16384], P('edp', 'ep')
Inputs may be any that keep to these rules, and one draw needn't show every extreme that they name: `routes`: each token names 8 different experts, at most one of them below 8. Among the tokens of one device no expert below 8 is named more than 8 times, and on every device one such expert, the same on all, is named exactly 8 times.
All inputs are finite; a program needn't handle non-finite values.
Results may differ from a plain program's by a relative error of at most 0.0029.
Values may be sent and summed in bfloat16 or wider, within the bound.
No kernel may reach another device: no remote copies, remote signals or barrier semaphores. Data moves between devices by JAX's collectives and lax.ppermute only.
A program may use at most 32 MiB of HBM per device.

v0:
```python
import jax
import jax.numpy as jnp
from jax import lax
from jax.sharding import PartitionSpec as P

CAP = 8
SHARDS = 8


def place_rows(out_grad, routes, gate_weights, experts):
    labels = jnp.arange(experts, dtype=jnp.int32)
    onehot = jnp.sum(
        (routes[:, :, None] == labels[None, None, :]).astype(jnp.int32), axis=1, dtype=jnp.int32
    )
    weight = jnp.sum(
        jnp.where(routes < experts, gate_weights, jnp.zeros_like(gate_weights)), axis=1
    )
    routed = (out_grad.astype(jnp.float32) * weight[:, None]).astype(jnp.bfloat16)
    slot_rank = jnp.cumsum(onehot, axis=0, dtype=jnp.int32) - onehot
    slot_index = jnp.sum(onehot * (labels[None, :] * CAP + slot_rank), axis=1, dtype=jnp.int32)
    is_live = jnp.sum(onehot, axis=1, dtype=jnp.int32)
    targets = jnp.arange(experts * CAP, dtype=jnp.int32)
    placer = ((is_live[None, :] == 1) & (slot_index[None, :] == targets[:, None])).astype(
        jnp.bfloat16
    )
    return jnp.dot(placer, routed, preferred_element_type=jnp.float32).astype(jnp.bfloat16)


def body(out_grad, routes, gate_weights, hidden):
    expert_devices = lax.axis_size("ep")
    experts = expert_devices // SHARDS
    features = out_grad.shape[1]
    outbound = place_rows(out_grad, routes, gate_weights, experts)
    outgoing = jnp.repeat(outbound.reshape(experts, CAP, features), SHARDS, axis=0)
    arrived = lax.all_to_all(outgoing, "ep", split_axis=0, concat_axis=0, tiled=True)
    slot_rows = arrived.reshape(-1, features)
    return lax.psum_scatter(
        lax.dot_general(
            slot_rows, hidden, (((0,), (0,)), ((), ())), preferred_element_type=jnp.float32
        ),
        "edp",
        scatter_dimension=0,
        tiled=True,
    )


def solution(mesh):
    return jax.shard_map(
        body,
        mesh=mesh,
        in_specs=(
            P(("edp", "ep"), None),
            P(("edp", "ep"), None),
            P(("edp", "ep"), None),
            P("edp", "ep"),
        ),
        out_specs=P("edp", "ep"),
        check_vma=False,
    )
```

profile of v0, /device:TPU:4, one launch (start us, length us, event | category | flops | bytes accessed | tf_op | source)
XLA Modules:
  0.0 201.5 jit_solution(4676475578845351915)
XLA Ops:
  6.5 0.0 copy-start
  6.5 0.0 reduce-scatter.2.cloned.1.call-start
  6.5 0.8 convert_reduce_fusion.1
  7.3 0.7 select_reduce_fusion
  8.0 0.1 copy.11
  8.1 0.2 reduce_window_sum.11
  8.3 0.1 multiply_reduce_fusion
  8.4 1.6 fusion
  10.0 0.3 broadcast_in_dim.5
  10.3 101.5 %all_to_all.5 = bf16[64,8,3584]{2,1,0:T(8,128)(2,1)S(1)} all-to-all(bf16[64,8,3584]{2,1,0:T(8,128)(2,1)S(1)} %bitcast.7), channel_id=1, replica_groups=mesh['edp'=16,'ep'=64] {'ep'}, dimensions={0} | all-to-all | bytes 7340032 | tf_op jit(solution)/shard_map/all_to_all | solution.py:35
  111.7 0.0 copy-done
  111.7 3.0 %fusion.1 = f32[3584,256]{1,0:T(8,128)} fusion(bf16[512,256]{1,0:T(8,128)(2,1)S(1)} %copy-done, bf16[64,8,3584]{2,1,0:T(8,128)(2,1)S(1)} %all_to_all.5), kind=kOutput, calls=%fused_computation.2 | convolution fusion | flops 939524096 | bytes 7602176 | tf_op jit(solution)/shard_map/dot_general | solution.py:38
  114.7 0.0 reduce-scatter.2.cloned.1.call-update
  114.7 79.9 %reduce-scatter.2.cloned.1.call-done = f32[224,256]{1,0:T(8,128)} async-done(((f32[3584,256]{1,0:T(8,128)}), f32[224,256]{1,0:T(8,128)}) %reduce-scatter.2.cloned.1.call-update) | async-done | bytes 229392 | tf_op jit(solution)/shard_map/reduce_scatter | solution.py:37
  (3 shorter events, 0.1 us)
Async XLA Ops:
  6.5 105.2 %copy-start = (bf16[512,256]{1,0:T(8,128)(2,1)S(1)}, bf16[512,256]{1,0:T(8,128)(2,1)}, u32[]{:S(2)}) copy-start(bf16[512,256]{1,0:T(8,128)(2,1)} %param.7) | copy-start | bytes 786436
  6.5 188.1 %reduce-scatter.2.cloned.1.call-start = ((), (), s32[]{:S(2)}) async-start(), calls=%async_computation.2 | async-start | bytes 3899392 | tf_op jit(solution)/shard_map/reduce_scatter | solution.py:37
Sparse Core Ops, SparseCore 0:
  114.8 79.7 reduce-scatter.1
where the time goes:
time: 202 us; the launch traced here: 201 us
  blocking collectives  101 us (50%)
  waiting for transfers between devices  79.9 us (40%)
  between operations  13.4 us (7%)
  matrix products  4.52 us (2%)
    all_to_all x1, blocking collectives, body(): lax.all_to_all(outgoing, 'ep', split_axis=0, concat_axis=0, tiled=True)  101 us
    reduce_scatter x1, waiting for transfers between devices, body(): lax.psum_scatter(lax.dot_general(slot_rows, hidden, (((0,), (0,)), ((), (...  79.9 us
  transfers between devices with their start and end apart: 1, of which 1 were waited for; matrix products, arithmetic and copies ran while one was open for 0% of the time, Pallas kernels for 0%

commit v1 on v0

v1 whole, which is shorter than its diff:
```python
import jax
import jax.numpy as jnp
from jax import lax
from jax.experimental import pallas as pl
from jax.sharding import Mesh, PartitionSpec as P

CAP = 8
EXPERTS = 8
GROUP = 4


def place_kernel(grad_ref, routes_ref, gates_ref, out_ref):
    tokens, features = grad_ref.shape
    block = features // (GROUP * GROUP)
    routes = routes_ref[...]
    local = routes < EXPERTS
    weight = jnp.sum(jnp.where(local, gates_ref[...], 0.0), axis=1, keepdims=True)
    expert = jnp.sum(jnp.where(local, routes + 1, 0), axis=1, keepdims=True) - 1
    onehot = expert == lax.broadcasted_iota(jnp.int32, (tokens, 128), 1)
    earlier = lax.broadcasted_iota(jnp.int32, (tokens, tokens), 1) < lax.broadcasted_iota(
        jnp.int32, (tokens, tokens), 0
    )
    ranks = jnp.dot(
        earlier.astype(jnp.float32).astype(jnp.bfloat16),
        onehot.astype(jnp.float32).astype(jnp.bfloat16),
        preferred_element_type=jnp.float32,
    )
    rank = jnp.sum(jnp.where(onehot, ranks, 0.0), axis=1, keepdims=True).astype(jnp.int32)
    slot = jnp.where(expert >= 0, expert * CAP + rank, -1)
    placer = (slot == lax.broadcasted_iota(jnp.int32, (tokens, EXPERTS * CAP), 1)).astype(
        jnp.float32
    ).astype(jnp.bfloat16)
    routed = (grad_ref[...].astype(jnp.float32) * weight).astype(jnp.bfloat16)
    placed = lax.dot_general(
        placer, routed, (((0,), (0,)), ((), ())), preferred_element_type=jnp.float32
    )
    for low in range(GROUP):
        picked = jnp.concatenate(
            [
                placed[:, (high * GROUP + low) * block : (high * GROUP + low + 1) * block]
                for high in range(GROUP)
            ],
            axis=1,
        )
        out_ref[low] = picked.astype(jnp.bfloat16).reshape(EXPERTS, CAP, GROUP * block)


def place_rows(out_grad, routes, gate_weights):
    features = out_grad.shape[1]
    return pl.pallas_call(
        place_kernel,
        out_shape=jax.ShapeDtypeStruct(
            (GROUP, EXPERTS, CAP, features // GROUP), jnp.bfloat16
        ),
        cost_estimate=pl.CostEstimate(
            flops=2 * 64 * 128 * features, bytes_accessed=3 * 64 * 2 * features, transcendentals=0
        ),
    )(out_grad, routes, gate_weights)


def gradient(out_grad, routes, gate_weights, hidden):
    columns = hidden.shape[1]
    low, core = lax.axis_index("zl"), lax.axis_index("c")
    mine = hidden.reshape(EXPERTS, GROUP, 2, CAP, columns).transpose(2, 1, 0, 3, 4)
    mine = mine.reshape(2, GROUP, EXPERTS * CAP, columns)
    gathered = [mine]
    for step in (1, 2, 3):
        gathered.append(lax.ppermute(mine, "zl", [(i, i ^ step) for i in range(GROUP)]))
    stacked = jnp.stack(gathered)
    saved = jnp.stack(
        [lax.dynamic_index_in_dim(stacked, low ^ source, 0, False) for source in range(GROUP)],
        axis=2,
    )
    saved = saved.reshape(2, -1, columns)

    outbound = place_rows(out_grad, routes, gate_weights)
    features = outbound.shape[-1]
    outbound = outbound.reshape(GROUP * EXPERTS, CAP, features)
    arrived = lax.all_to_all(outbound, ("zl", "y"), split_axis=0, concat_axis=0, tiled=True)
    arrived = jnp.broadcast_to(
        arrived.reshape(1, -1, features), (GROUP, GROUP * EXPERTS * CAP, features)
    )
    rows = lax.all_to_all(arrived, "x", split_axis=0, concat_axis=0, tiled=True)
    rows = rows.reshape(-1, features)
    others = lax.ppermute(rows, "c", [(0, 1), (1, 0)])

    def product(part, which):
        return lax.dot_general(
            part,
            lax.dynamic_index_in_dim(saved, which, 0, False),
            (((0,), (0,)), ((), ())),
            preferred_element_type=jnp.float32,
        )

    partial = product(rows, core) + product(others, 1 - core)
    partial = partial.astype(jnp.bfloat16).reshape(GROUP, features // GROUP, columns)
    parts = lax.all_to_all(partial, "zh", split_axis=0, concat_axis=0, tiled=True)
    return jnp.sum(parts.astype(jnp.float32), axis=0)


def solution(mesh):
    axes = ("zh", "zl", "y", "x", "c")
    fine = Mesh(mesh.devices.reshape(GROUP, GROUP, EXPERTS, 4, 2), axes)
    tokens = P(axes, None)
    return jax.shard_map(
        gradient,
        mesh=fine,
        in_specs=(tokens, tokens, tokens, P(("zh", "zl"), ("y", "x", "c"))),
        out_specs=P(("zh", "zl"), ("y", "x", "c")),
        check_vma=False,
    )
```

time: 202 us -> 137 us (0.68)
  the two profiles are of different devices: /device:TPU:4 before, /device:TPU:8 now
where the time goes in v1:
time: 137 us; the launch traced here: 136 us
  blocking collectives  99.5 us (73%)
  waiting for transfers between devices  14.2 us (10%)
  starting transfers between devices  12.7 us (9%)
  local copies, waits for them, and re-layouts  3.09 us (2%)
  matrix products  2.88 us (2%)
  Pallas kernels  2.73 us (2%)
    all_to_all x1, blocking collectives, gradient(): lax.all_to_all(partial, 'zh', split_axis=0, concat_axis=0, tiled=True)  45.6 us
    all_to_all x1, blocking collectives, gradient(): lax.all_to_all(outbound, ('zl', 'y'), split_axis=0, concat_axis=0, tiled=...  28.9 us
    all_to_all x1, blocking collectives, gradient(): rows = lax.all_to_all(arrived, 'x', split_axis=0, concat_axis=0, tiled=True)  25.1 us
    ppermute x3, waiting for transfers between devices, gradient(): lax.ppermute(mine, 'zl', [(i, i ^ step) for i in range(GROUP)])  14.2 us
    ppermute x3, starting transfers between devices, gradient(): lax.ppermute(mine, 'zl', [(i, i ^ step) for i in range(GROUP)])  10.8 us
    dot_general x2, matrix products, product(): lax.dot_general(part, lax.dynamic_index_in_dim(saved, which, 0, False), (...  2.88 us
    unnamed x4, local copies, waits for them, and re-layouts  2.83 us
  transfers between devices with their start and end apart: 4, of which 3 were waited for; matrix products, arithmetic and copies ran while one was open for 1% of the time, Pallas kernels for 0%

profile of v1, /device:TPU:8, one launch (start us, length us, event | category | flops | bytes accessed | tf_op | source)
XLA Modules:
  0.0 136.2 jit_solution(3599530120215803055)
XLA Ops:
  0.0 1.4 %copy.9.routes_ref = s32[128,8]{1,0:T(8,128)} copy(s32[128,8]{0,1:T(8,128)} %param.5) | data formatting | bytes 8192 | tf_op args[1]
  1.4 1.4 %copy.10.gates_ref = f32[128,8]{1,0:T(8,128)} copy(f32[128,8]{0,1:T(8,128)} %param.6) | data formatting | bytes 8192 | tf_op args[2]
  2.8 2.7 %shard_map.46 = bf16[4,8,8,896]{3,2,1,0:T(8,128)(2,1)} custom-call(bf16[128,3584]{1,0:T(8,128)(2,1)} %grad_ref.1, s32[128,8]{1,0:T(8,128)} %copy.9.routes_ref, f32[128,8]{1,0:T(8,128)} %copy.10.gates_ref), custom_call_target="tpu_custom_call" | custom-call | flops 58720256 | bytes 1376256 | tf_op jit(solution)/shard_map/pallas_call | solution.py:50
  5.6 28.9 %all_to_all.15 = bf16[32,8,896]{2,1,0:T(8,128)(2,1)S(1)} all-to-all(bf16[32,8,896]{2,1,0:T(8,128)(2,1)} %bitcast.34), channel_id=1, replica_groups=mesh['zh'=4,'zl'=4,'y'=8,'x'=4,'c'=2] {'zl','y'}, dimensions={0} | all-to-all | bytes 917504 | tf_op jit(solution)/shard_map/all_to_all | solution.py:79
  34.5 0.1 broadcast_in_dim.8
  34.6 0.0 copy-start
  34.6 25.1 %all_to_all.16 = bf16[4,256,896]{2,1,0:T(8,128)(2,1)S(1)} all-to-all(bf16[4,256,896]{2,1,0:T(8,128)(2,1)S(1)} %broadcast_in_dim.8), channel_id=1, replica_groups=mesh['zh'=4,'zl'=4,'y'=8,'x'=4,'c'=2] {'x'}, dimensions={0} | all-to-all | bytes 3670016 | tf_op jit(solution)/shard_map/all_to_all | solution.py:83
  59.7 1.9 %collective-permute-start.3 = (bf16[1024,896]{1,0:T(8,128)(2,1)S(1)}, bf16[1024,896]{1,0:T(8,128)(2,1)}, u32[]{:S(2)}, u32[]{:S(2)}) collective-permute-start(bf16[1024,896]{1,0:T(8,128)(2,1)S(1)} %bitcast.32), channel_id=1, source_target_pairs={{0,1},{1,0},{2,3},{3,2},{4,5},{5,4},{6,7},{7,6},{8,9},{9,8},{10,11... | collective-permute-start | bytes 5505032 | tf_op jit(solution)/shard_map/ppermute | solution.py:85
  61.6 0.0 copy-done
  61.6 4.3 %collective-permute-start.1 = (bf16[2,4,64,256]{3,2,1,0:T(8,128)(2,1)S(1)}, bf16[2,4,64,256]{3,2,1,0:T(8,128)(2,1)S(1)}, u32[]{:S(2)}, u32[]{:S(2)}) collective-permute-start(bf16[2,4,64,256]{3,2,1,0:T(8,128)(2,1)S(1)} %bitcast.38), channel_id=1, source_target_pairs={{0,128},{64,192},{128,0},{192,64},{1,129},{65,193},{129,1},{193,65... | collective-permute-start | bytes 786440 | tf_op jit(solution)/shard_map/ppermute | solution.py:68
  66.0 4.0 %collective-permute-start = (bf16[2,4,64,256]{3,2,1,0:T(8,128)(2,1)S(1)}, bf16[2,4,64,256]{3,2,1,0:T(8,128)(2,1)S(1)}, u32[]{:S(2)}, u32[]{:S(2)}) collective-permute-start(bf16[2,4,64,256]{3,2,1,0:T(8,128)(2,1)S(1)} %bitcast.39), channel_id=1, source_target_pairs={{0,64},{64,0},{128,192},{192,128},{1,65},{65,1},{129,193},{193,129... | collective-permute-start | bytes 786440 | tf_op jit(solution)/shard_map/ppermute | solution.py:68
  70.0 2.5 %collective-permute-start.2 = (bf16[2,4,64,256]{3,2,1,0:T(8,128)(2,1)S(1)}, bf16[2,4,64,256]{3,2,1,0:T(8,128)(2,1)S(1)}, u32[]{:S(2)}, u32[]{:S(2)}) collective-permute-start(bf16[2,4,64,256]{3,2,1,0:T(8,128)(2,1)S(1)} %bitcast.40), channel_id=1, source_target_pairs={{0,192},{64,128},{128,64},{192,0},{1,193},{65,129},{129,65},{193,1... | collective-permute-start | bytes 786440 | tf_op jit(solution)/shard_map/ppermute | solution.py:68
  72.5 6.8 %collective-permute-done.1 = bf16[2,4,64,256]{3,2,1,0:T(8,128)(2,1)S(1)} collective-permute-done((bf16[2,4,64,256]{3,2,1,0:T(8,128)(2,1)S(1)}, bf16[2,4,64,256]{3,2,1,0:T(8,128)(2,1)S(1)}, u32[]{:S(2)}, u32[]{:S(2)}) %collective-permute-start.1) | collective-permute-done | bytes 262176 | tf_op jit(solution)/shard_map/ppermute | solution.py:68
  79.3 0.8 collective-permute-done
  80.1 6.6 %collective-permute-done.2 = bf16[2,4,64,256]{3,2,1,0:T(8,128)(2,1)S(1)} collective-permute-done((bf16[2,4,64,256]{3,2,1,0:T(8,128)(2,1)S(1)}, bf16[2,4,64,256]{3,2,1,0:T(8,128)(2,1)S(1)}, u32[]{:S(2)}, u32[]{:S(2)}) %collective-permute-start.2) | collective-permute-done | bytes 262176 | tf_op jit(solution)/shard_map/ppermute | solution.py:68
  86.6 0.1 pad_maximum_fusion
  86.8 0.1 dynamic-slice_bitcast_fusion.3
  86.9 0.1 pad_maximum_fusion.1
  87.0 0.7 fusion.2
  87.7 0.0 collective-permute-done.3
  87.7 2.2 %fusion = bf16[896,256]{1,0:T(8,128)(2,1)S(1)} fusion(f32[896,256]{1,0:T(8,128)S(1)} %fusion.2, bf16[1024,896]{1,0:T(8,128)(2,1)} %collective-permute-done.3, bf16[2,1024,256]{2,1,0:T(8,128)(2,1)S(1)} %bitcast.37, s32[]{:T(128)S(6)} %select_n.25), kind=kOutput, calls=%fused_computation.1 | convolution fusion | flops 470220800 | bytes 3735556 | tf_op jit(solution)/shard_map/dot_general | solution.py:88
  89.9 45.6 %all_to_all.17 = bf16[4,224,256]{2,1,0:T(8,128)(2,1)S(1)} all-to-all(bf16[4,224,256]{2,1,0:T(8,128)(2,1)S(1)} %bitcast.42), channel_id=1, replica_groups=mesh['zh'=4,'zl'=4,'y'=8,'x'=4,'c'=2] {'zh'}, dimensions={0} | all-to-all | bytes 917504 | tf_op jit(solution)/shard_map/all_to_all | solution.py:97
  135.5 0.7 convert_reduce_fusion
  (1 shorter events, 0.0 us)
Async XLA Ops:
  34.6 27.0 %copy-start = (bf16[512,256]{1,0:T(8,128)(2,1)S(1)}, bf16[512,256]{1,0:T(8,128)(2,1)}, u32[]{:S(2)}) copy-start(bf16[512,256]{1,0:T(8,128)(2,1)} %param.7) | copy-start | bytes 786436
  59.7 28.0 %collective-permute-start.3 = (bf16[1024,896]{1,0:T(8,128)(2,1)S(1)}, bf16[1024,896]{1,0:T(8,128)(2,1)}, u32[]{:S(2)}, u32[]{:S(2)}) collective-permute-start(bf16[1024,896]{1,0:T(8,128)(2,1)S(1)} %bitcast.32), channel_id=1, source_target_pairs={{0,1},{1,0},{2,3},{3,2},{4,5},{5,4},{6,7},{7,6},{8,9},{9,8},{10,11... | collective-permute-start | bytes 5505032 | tf_op jit(solution)/shard_map/ppermute | solution.py:85
  61.6 17.6 %collective-permute-start.1 = (bf16[2,4,64,256]{3,2,1,0:T(8,128)(2,1)S(1)}, bf16[2,4,64,256]{3,2,1,0:T(8,128)(2,1)S(1)}, u32[]{:S(2)}, u32[]{:S(2)}) collective-permute-start(bf16[2,4,64,256]{3,2,1,0:T(8,128)(2,1)S(1)} %bitcast.38), channel_id=1, source_target_pairs={{0,128},{64,192},{128,0},{192,64},{1,129},{65,193},{129,1},{193,65... | collective-permute-start | bytes 786440 | tf_op jit(solution)/shard_map/ppermute | solution.py:68
  66.0 14.1 %collective-permute-start = (bf16[2,4,64,256]{3,2,1,0:T(8,128)(2,1)S(1)}, bf16[2,4,64,256]{3,2,1,0:T(8,128)(2,1)S(1)}, u32[]{:S(2)}, u32[]{:S(2)}) collective-permute-start(bf16[2,4,64,256]{3,2,1,0:T(8,128)(2,1)S(1)} %bitcast.39), channel_id=1, source_target_pairs={{0,64},{64,0},{128,192},{192,128},{1,65},{65,1},{129,193},{193,129... | collective-permute-start | bytes 786440 | tf_op jit(solution)/shard_map/ppermute | solution.py:68
  70.0 16.7 %collective-permute-start.2 = (bf16[2,4,64,256]{3,2,1,0:T(8,128)(2,1)S(1)}, bf16[2,4,64,256]{3,2,1,0:T(8,128)(2,1)S(1)}, u32[]{:S(2)}, u32[]{:S(2)}) collective-permute-start(bf16[2,4,64,256]{3,2,1,0:T(8,128)(2,1)S(1)} %bitcast.40), channel_id=1, source_target_pairs={{0,192},{64,128},{128,64},{192,0},{1,193},{65,129},{129,65},{193,1... | collective-permute-start | bytes 786440 | tf_op jit(solution)/shard_map/ppermute | solution.py:68

commit v2 on v1

--- a/solution.py
+++ b/solution.py
@@ -14,26 +14,25 @@
     block = features // (GROUP * GROUP)
     routes = routes_ref[...]
     local = routes < EXPERTS
-    weight = jnp.sum(jnp.where(local, gates_ref[...], 0.0), axis=1, keepdims=True)
-    expert = jnp.sum(jnp.where(local, routes + 1, 0), axis=1, keepdims=True) - 1
-    onehot = expert == lax.broadcasted_iota(jnp.int32, (tokens, 128), 1)
-    earlier = lax.broadcasted_iota(jnp.int32, (tokens, tokens), 1) < lax.broadcasted_iota(
-        jnp.int32, (tokens, tokens), 0
+    weight = jnp.sum(jnp.where(local, gates_ref[...], 0.0), axis=0, keepdims=True)
+    weight = jnp.transpose(jnp.broadcast_to(weight, (8, tokens)))[:, :1]
+    expert = jnp.sum(jnp.where(local, routes + 1, 0), axis=0, keepdims=True) - 1
+    onehot = expert == lax.broadcasted_iota(jnp.int32, (EXPERTS, tokens), 0)
+    earlier = lax.broadcasted_iota(jnp.int32, (tokens, tokens), 0) < lax.broadcasted_iota(
+        jnp.int32, (tokens, tokens), 1
     )
     ranks = jnp.dot(
+        onehot.astype(jnp.float32).astype(jnp.bfloat16),
         earlier.astype(jnp.float32).astype(jnp.bfloat16),
-        onehot.astype(jnp.float32).astype(jnp.bfloat16),
         preferred_element_type=jnp.float32,
     )
-    rank = jnp.sum(jnp.where(onehot, ranks, 0.0), axis=1, keepdims=True).astype(jnp.int32)
+    rank = jnp.sum(jnp.where(onehot, ranks, 0.0), axis=0, keepdims=True).astype(jnp.int32)
     slot = jnp.where(expert >= 0, expert * CAP + rank, -1)
-    placer = (slot == lax.broadcasted_iota(jnp.int32, (tokens, EXPERTS * CAP), 1)).astype(
+    placer = (slot == lax.broadcasted_iota(jnp.int32, (EXPERTS * CAP, tokens), 0)).astype(
         jnp.float32
     ).astype(jnp.bfloat16)
     routed = (grad_ref[...].astype(jnp.float32) * weight).astype(jnp.bfloat16)
-    placed = lax.dot_general(
-        placer, routed, (((0,), (0,)), ((), ())), preferred_element_type=jnp.float32
-    )
+    placed = jnp.dot(placer, routed, preferred_element_type=jnp.float32)
     for low in range(GROUP):
         picked = jnp.concatenate(
             [
@@ -55,12 +54,16 @@
         cost_estimate=pl.CostEstimate(
             flops=2 * 64 * 128 * features, bytes_accessed=3 * 64 * 2 * features, transcendentals=0
         ),
-    )(out_grad, routes, gate_weights)
+    )(out_grad, routes.T, gate_weights.T)
 
 
 def gradient(out_grad, routes, gate_weights, hidden):
     columns = hidden.shape[1]
     low, core = lax.axis_index("zl"), lax.axis_index("c")
+    outbound = place_rows(out_grad, routes, gate_weights)
+    features = outbound.shape[-1]
+    outbound = outbound.reshape(GROUP * EXPERTS, CAP, features)
+    arrived = lax.all_to_all(outbound, ("zl", "y"), split_axis=0, concat_axis=0, tiled=True)
     mine = hidden.reshape(EXPERTS, GROUP, 2, CAP, columns).transpose(2, 1, 0, 3, 4)
     mine = mine.reshape(2, GROUP, EXPERTS * CAP, columns)
     gathered = [mine]
@@ -73,10 +76,6 @@
     )
     saved = saved.reshape(2, -1, columns)
 
-    outbound = place_rows(out_grad, routes, gate_weights)
-    features = outbound.shape[-1]
-    outbound = outbound.reshape(GROUP * EXPERTS, CAP, features)
-    arrived = lax.all_to_all(outbound, ("zl", "y"), split_axis=0, concat_axis=0, tiled=True)
     arrived = jnp.broadcast_to(
         arrived.reshape(1, -1, features), (GROUP, GROUP * EXPERTS * CAP, features)
     )

time: 137 us -> 133 us (0.971)
  the two profiles are of different devices: /device:TPU:8 before, /device:TPU:65 now
where the time goes in v2:
time: 133 us
  blocking collectives  92 us (69%)
  waiting for transfers between devices  17.9 us (13%)
  starting transfers between devices  16 us (12%)
  matrix products  2.88 us (2%)
  Pallas kernels  2.55 us (2%)
    all_to_all x1, blocking collectives, gradient(): lax.all_to_all(partial, 'zh', split_axis=0, concat_axis=0, tiled=True)  42.6 us
    all_to_all x1, blocking collectives, gradient(): rows = lax.all_to_all(arrived, 'x', split_axis=0, concat_axis=0, tiled=True)  27.4 us
    all_to_all x1, blocking collectives, gradient(): lax.all_to_all(outbound, ('zl', 'y'), split_axis=0, concat_axis=0, tiled=...  22 us
    ppermute x3, waiting for transfers between devices, gradient(): lax.ppermute(mine, 'zl', [(i, i ^ step) for i in range(GROUP)])  17.9 us
    ppermute x3, starting transfers between devices, gradient(): lax.ppermute(mine, 'zl', [(i, i ^ step) for i in range(GROUP)])  9.87 us
    ppermute x1, starting transfers between devices, gradient(): others = lax.ppermute(rows, 'c', [(0, 1), (1, 0)])  6.13 us
    dot_general x2, matrix products, product(): lax.dot_general(part, lax.dynamic_index_in_dim(saved, which, 0, False), (...  2.88 us
  transfers between devices with their start and end apart: 4, of which 3 were waited for; matrix products, arithmetic and copies ran while one was open for 1% of the time, Pallas kernels for 0%

profile of v2, /device:TPU:65, one launch (start us, length us, event | category | flops | bytes accessed | tf_op | source)
XLA Modules:
  0.0 132.8 jit_solution(11246115179577095223)
XLA Ops:
  0.0 2.5 %shard_map.46 = bf16[4,8,8,896]{3,2,1,0:T(8,128)(2,1)} custom-call(bf16[128,3584]{1,0:T(8,128)(2,1)} %grad_ref.1, s32[8,128]{1,0:T(8,128)} %bitcast.49, f32[8,128]{1,0:T(8,128)} %bitcast.50), custom_call_target="tpu_custom_call" | custom-call | flops 58720256 | bytes 1376256 | tf_op jit(solution)/shard_map/pallas_call | solution.py:49
  2.5 22.0 %all_to_all.15 = bf16[32,8,896]{2,1,0:T(8,128)(2,1)S(1)} all-to-all(bf16[32,8,896]{2,1,0:T(8,128)(2,1)} %bitcast.37), channel_id=1, replica_groups=mesh['zh'=4,'zl'=4,'y'=8,'x'=4,'c'=2] {'zl','y'}, dimensions={0} | all-to-all | bytes 917504 | tf_op jit(solution)/shard_map/all_to_all | solution.py:66
  24.6 0.1 broadcast_in_dim.8
  24.7 0.0 copy-start
  24.7 27.4 %all_to_all.16 = bf16[4,256,896]{2,1,0:T(8,128)(2,1)S(1)} all-to-all(bf16[4,256,896]{2,1,0:T(8,128)(2,1)S(1)} %broadcast_in_dim.8), channel_id=1, replica_groups=mesh['zh'=4,'zl'=4,'y'=8,'x'=4,'c'=2] {'x'}, dimensions={0} | all-to-all | bytes 3670016 | tf_op jit(solution)/shard_map/all_to_all | solution.py:82
  52.1 6.1 %collective-permute-start.3 = (bf16[1024,896]{1,0:T(8,128)(2,1)S(1)}, bf16[1024,896]{1,0:T(8,128)(2,1)}, u32[]{:S(2)}, u32[]{:S(2)}) collective-permute-start(bf16[1024,896]{1,0:T(8,128)(2,1)S(1)} %bitcast.34), channel_id=1, source_target_pairs={{0,1},{1,0},{2,3},{3,2},{4,5},{5,4},{6,7},{7,6},{8,9},{9,8},{10,11... | collective-permute-start | bytes 5505032 | tf_op jit(solution)/shard_map/ppermute | solution.py:84
  58.2 0.0 copy-done
  58.3 5.8 %collective-permute-start.1 = (bf16[2,4,64,256]{3,2,1,0:T(8,128)(2,1)S(1)}, bf16[2,4,64,256]{3,2,1,0:T(8,128)(2,1)S(1)}, u32[]{:S(2)}, u32[]{:S(2)}) collective-permute-start(bf16[2,4,64,256]{3,2,1,0:T(8,128)(2,1)S(1)} %bitcast.40), channel_id=1, source_target_pairs={{0,128},{64,192},{128,0},{192,64},{1,129},{65,193},{129,1},{193,65... | collective-permute-start | bytes 786440 | tf_op jit(solution)/shard_map/ppermute | solution.py:71
  64.0 1.9 %collective-permute-start = (bf16[2,4,64,256]{3,2,1,0:T(8,128)(2,1)S(1)}, bf16[2,4,64,256]{3,2,1,0:T(8,128)(2,1)S(1)}, u32[]{:S(2)}, u32[]{:S(2)}) collective-permute-start(bf16[2,4,64,256]{3,2,1,0:T(8,128)(2,1)S(1)} %bitcast.41), channel_id=1, source_target_pairs={{0,64},{64,0},{128,192},{192,128},{1,65},{65,1},{129,193},{193,129... | collective-permute-start | bytes 786440 | tf_op jit(solution)/shard_map/ppermute | solution.py:71
  66.0 2.2 %collective-permute-start.2 = (bf16[2,4,64,256]{3,2,1,0:T(8,128)(2,1)S(1)}, bf16[2,4,64,256]{3,2,1,0:T(8,128)(2,1)S(1)}, u32[]{:S(2)}, u32[]{:S(2)}) collective-permute-start(bf16[2,4,64,256]{3,2,1,0:T(8,128)(2,1)S(1)} %bitcast.42), channel_id=1, source_target_pairs={{0,192},{64,128},{128,64},{192,0},{1,193},{65,129},{129,65},{193,1... | collective-permute-start | bytes 786440 | tf_op jit(solution)/shard_map/ppermute | solution.py:71
  68.2 6.6 %collective-permute-done.1 = bf16[2,4,64,256]{3,2,1,0:T(8,128)(2,1)S(1)} collective-permute-done((bf16[2,4,64,256]{3,2,1,0:T(8,128)(2,1)S(1)}, bf16[2,4,64,256]{3,2,1,0:T(8,128)(2,1)S(1)}, u32[]{:S(2)}, u32[]{:S(2)}) %collective-permute-start.1) | collective-permute-done | bytes 262176 | tf_op jit(solution)/shard_map/ppermute | solution.py:71
  74.8 0.6 collective-permute-done
  75.5 10.7 %collective-permute-done.2 = bf16[2,4,64,256]{3,2,1,0:T(8,128)(2,1)S(1)} collective-permute-done((bf16[2,4,64,256]{3,2,1,0:T(8,128)(2,1)S(1)}, bf16[2,4,64,256]{3,2,1,0:T(8,128)(2,1)S(1)}, u32[]{:S(2)}, u32[]{:S(2)}) %collective-permute-start.2) | collective-permute-done | bytes 262176 | tf_op jit(solution)/shard_map/ppermute | solution.py:71
  86.1 0.1 pad_maximum_fusion
  86.2 0.1 dynamic-slice_bitcast_fusion.3
  86.4 0.1 pad_maximum_fusion.1
  86.5 0.7 fusion.2
  87.2 0.0 collective-permute-done.3
  87.2 2.2 %fusion = bf16[896,256]{1,0:T(8,128)(2,1)S(1)} fusion(f32[896,256]{1,0:T(8,128)S(1)} %fusion.2, bf16[1024,896]{1,0:T(8,128)(2,1)} %collective-permute-done.3, bf16[2,1024,256]{2,1,0:T(8,128)(2,1)S(1)} %bitcast.39, s32[]{:T(128)S(6)} %select_n.25), kind=kOutput, calls=%fused_computation.1 | convolution fusion | flops 470220800 | bytes 3735556 | tf_op jit(solution)/shard_map/dot_general | solution.py:87
  89.4 42.6 %all_to_all.17 = bf16[4,224,256]{2,1,0:T(8,128)(2,1)S(1)} all-to-all(bf16[4,224,256]{2,1,0:T(8,128)(2,1)S(1)} %bitcast.44), channel_id=1, replica_groups=mesh['zh'=4,'zl'=4,'y'=8,'x'=4,'c'=2] {'zh'}, dimensions={0} | all-to-all | bytes 917504 | tf_op jit(solution)/shard_map/all_to_all | solution.py:96
  132.0 0.7 convert_reduce_fusion
  (1 shorter events, 0.0 us)
Async XLA Ops:
  24.7 33.5 %copy-start = (bf16[512,256]{1,0:T(8,128)(2,1)S(1)}, bf16[512,256]{1,0:T(8,128)(2,1)}, u32[]{:S(2)}) copy-start(bf16[512,256]{1,0:T(8,128)(2,1)} %param.7) | copy-start | bytes 786436
  52.1 35.1 %collective-permute-start.3 = (bf16[1024,896]{1,0:T(8,128)(2,1)S(1)}, bf16[1024,896]{1,0:T(8,128)(2,1)}, u32[]{:S(2)}, u32[]{:S(2)}) collective-permute-start(bf16[1024,896]{1,0:T(8,128)(2,1)S(1)} %bitcast.34), channel_id=1, source_target_pairs={{0,1},{1,0},{2,3},{3,2},{4,5},{5,4},{6,7},{7,6},{8,9},{9,8},{10,11... | collective-permute-start | bytes 5505032 | tf_op jit(solution)/shard_map/ppermute | solution.py:84
  58.3 16.5 %collective-permute-start.1 = (bf16[2,4,64,256]{3,2,1,0:T(8,128)(2,1)S(1)}, bf16[2,4,64,256]{3,2,1,0:T(8,128)(2,1)S(1)}, u32[]{:S(2)}, u32[]{:S(2)}) collective-permute-start(bf16[2,4,64,256]{3,2,1,0:T(8,128)(2,1)S(1)} %bitcast.40), channel_id=1, source_target_pairs={{0,128},{64,192},{128,0},{192,64},{1,129},{65,193},{129,1},{193,65... | collective-permute-start | bytes 786440 | tf_op jit(solution)/shard_map/ppermute | solution.py:71
  64.0 11.4 %collective-permute-start = (bf16[2,4,64,256]{3,2,1,0:T(8,128)(2,1)S(1)}, bf16[2,4,64,256]{3,2,1,0:T(8,128)(2,1)S(1)}, u32[]{:S(2)}, u32[]{:S(2)}) collective-permute-start(bf16[2,4,64,256]{3,2,1,0:T(8,128)(2,1)S(1)} %bitcast.41), channel_id=1, source_target_pairs={{0,64},{64,0},{128,192},{192,128},{1,65},{65,1},{129,193},{193,129... | collective-permute-start | bytes 786440 | tf_op jit(solution)/shard_map/ppermute | solution.py:71
  66.0 20.1 %collective-permute-start.2 = (bf16[2,4,64,256]{3,2,1,0:T(8,128)(2,1)S(1)}, bf16[2,4,64,256]{3,2,1,0:T(8,128)(2,1)S(1)}, u32[]{:S(2)}, u32[]{:S(2)}) collective-permute-start(bf16[2,4,64,256]{3,2,1,0:T(8,128)(2,1)S(1)} %bitcast.42), channel_id=1, source_target_pairs={{0,192},{64,128},{128,64},{192,0},{1,193},{65,129},{129,65},{193,1... | collective-permute-start | bytes 786440 | tf_op jit(solution)/shard_map/ppermute | solution.py:71
